TPU v7x, 128 devices: a whole 4x4x4 slice. The times are simulated.
128 devices in a mesh: attn: 4 (over x), expert: 32 (over z, y, core).
Axes of the slice: x: 4, y: 4, z: 4, core: 2. Of those that a mesh axis runs over, the one named last changes fastest.
Arguments:
- tokens: bfloat16 [4096, 2880], P(('attn', 'expert')), may hold values from -6 to 6
- expert_ids: int32 [4096, 4], P(('attn', 'expert')), may hold values from 0 to 31, all different within a row; in each aligned block of 32 rows (0 to 31, 32 to 63, ...) at most 12 rows name the same one
- gate_probs: float32 [4096, 4], P(('attn', 'expert')), may hold values from 0.05 to 0.6
- shed_blocks: int32 [32], replicated, may hold values from 0 to 4, as said below
- partner: int32 [32], replicated, may hold values from 0 to 31, as said below
- gate_weight: bfloat16 [32, 2880, 2880], P('expert', None, 'attn'), may hold values from -0.109375 to 0.109375
- up_weight: bfloat16 [32, 2880, 2880], P('expert', None, 'attn'), may hold values from -0.109375 to 0.109375
- down_weight: bfloat16 [32, 2880, 2880], P('expert', 'attn'), may hold values from -0.109375 to 0.109375
Outputs:
- moe_out: bfloat16 [4096, 2880], P(('attn', 'expert'))
Inputs may be any that keep to these rules, and one draw needn't show every extreme that they name: `expert_ids`: in the rows of one device, no expert is named by more than 12 rows; the 4 experts of a token differ. `shed_blocks`: some expert has exactly 4. partner pairs the experts: partner[partner[e]] = e and partner[e] != e.
All inputs are finite; a program needn't handle non-finite values.
Results may differ from a plain program's by a relative error of at most 0.0081.
Values may be sent and summed in bfloat16 or wider, within the bound.
No kernel may reach another device: no remote copies, remote signals or barrier semaphores. Data moves between devices by JAX's collectives and lax.ppermute only.
A program may use at most 128 MiB of HBM per device.

v0:
```python
import jax
import jax.numpy as jnp
from jax import lax
from jax.sharding import Mesh
from jax.sharding import PartitionSpec as P

SHED_MOST = 4
ATTN_EXPERT = ("attn", "expert_0", "expert_1", "expert_2")
EXPERT = ("expert_0", "expert_1", "expert_2")
SWISH_SCALE = 1.702


def nothing_yet(array, identity):
    return jnp.broadcast_to(jnp.asarray(identity, array.dtype), array.shape)


def prefix_by_axis(array, axes, combine, identity):
    before = start = nothing_yet(array, identity)
    total = array
    for axis in reversed(axes):
        devices, mine = (lax.axis_size(axis), lax.axis_index(axis))
        pieces = lax.all_gather(total, axis)
        inside, total = (start, start)
        for k in range(devices):
            passed = k < mine
            total = combine(total, pieces[k])
            inside = jnp.where(passed, total, inside)
        before = combine(inside, before)
    return before


def split_up(array, dim, devices):
    dims = array.shape
    parts = array.reshape(*dims[:dim], devices, dims[dim] // devices, *dims[dim + 1 :])
    return jnp.moveaxis(parts, dim, 0)


def sum_at_owner(array, axis, dim):
    parts = split_up(array, dim, lax.axis_size(axis))
    arrived = lax.all_to_all(parts, axis, split_axis=0, concat_axis=0, tiled=True)
    return arrived.astype(jnp.float32).sum(axis=0)


def lookup(table, indices):
    places = jnp.arange(table.shape[0], dtype=jnp.int32)
    return jnp.sum(jnp.where(indices[:, None] == places[None, :], table[None, :], 0), axis=1)


def add_counts(earlier, later):
    return earlier + later


def activate(rows, gate_w, up_w):
    gate_part = jnp.dot(rows, gate_w, preferred_element_type=jnp.float32)
    up_part = jnp.dot(rows, up_w, preferred_element_type=jnp.float32)
    return (gate_part * jax.nn.sigmoid(SWISH_SCALE * gate_part) * (up_part + 1.0)).astype(
        jnp.bfloat16
    )


def on_device(
    tokens, expert_ids, gate_probs, shed_blocks, partner, gate_weight, up_weight, down_weight
):
    tok_rows, model_width = tokens.shape
    top_count = expert_ids.shape[1]
    expert_count = shed_blocks.shape[0]
    group_count = lax.axis_size("attn")
    capacity = tok_rows * top_count * group_count
    block_size = capacity // 8
    most_rows = min(tok_rows, 3 * tok_rows * top_count // expert_count)
    slot_count = 2 * most_rows
    places = jnp.arange(expert_count, dtype=jnp.int32)
    flat_ids = expert_ids.reshape(-1)
    onehot = (flat_ids[:, None] == places[None, :]).astype(jnp.int32)
    counts = jnp.sum(onehot, axis=0)
    local_rank = jnp.sum((jnp.cumsum(onehot, axis=0) - onehot) * onehot, axis=1)
    offsets = prefix_by_axis(counts, ATTN_EXPERT, add_counts, jnp.zeros_like(counts))
    global_rank = local_rank + jnp.sum(onehot * offsets[None, :], axis=1)
    limit = capacity - block_size * lookup(shed_blocks, partner)
    own_limit = lookup(limit, flat_ids)
    own_shed = lookup(shed_blocks, flat_ids)
    native = global_rank < own_limit
    borrowed = jnp.logical_and(
        jnp.logical_not(native), global_rank < own_limit + block_size * own_shed
    )
    usable = jnp.logical_or(native, borrowed)
    target = jnp.where(usable, flat_ids, -1)
    table_rows = capacity + block_size * SHED_MOST
    target_hot = (target[:, None] == places[None, :]).astype(jnp.int32)
    position = jnp.sum((jnp.cumsum(target_hot, axis=0) - target_hot) * target_hot, axis=1)
    buffer_index = jnp.where(usable, target * slot_count + position, expert_count * slot_count)
    token_rows = jnp.repeat(tokens, top_count, axis=0)
    send_rows = (
        jnp.zeros((expert_count * slot_count, model_width), jnp.bfloat16)
        .at[buffer_index]
        .set(token_rows, mode="drop")
    )
    send_slots = (
        jnp.full((expert_count * slot_count,), table_rows, jnp.int32)
        .at[buffer_index]
        .set(global_rank, mode="drop")
    )
    send_rows = send_rows.reshape(expert_count, slot_count, model_width)
    send_slots = send_slots.reshape(expert_count, slot_count)
    got_rows, got_slots = (
        lax.all_to_all(send_rows, EXPERT, split_axis=0, concat_axis=0, tiled=True),
        lax.all_to_all(send_slots, EXPERT, split_axis=0, concat_axis=0, tiled=True),
    )
    local_table = (
        jnp.zeros((table_rows, model_width), jnp.float32)
        .at[got_slots.reshape(-1)]
        .set(got_rows.reshape(-1, model_width).astype(jnp.float32), mode="drop")
    )
    compact = lax.psum(local_table.astype(jnp.bfloat16), "attn")
    gate_own = gate_weight[0]
    up_own = up_weight[0]
    down_own = down_weight[0]
    hidden_own = activate(compact, gate_own, up_own)
    share = sum_at_owner(
        jnp.dot(hidden_own, down_own, preferred_element_type=jnp.float32).astype(jnp.bfloat16),
        "attn",
        0,
    )
    results = lax.all_gather(share.astype(jnp.bfloat16), "attn", axis=0, tiled=True)
    answers = results[jnp.minimum(got_slots, table_rows - 1)]
    returned = lax.all_to_all(answers, EXPERT, split_axis=0, concat_axis=0, tiled=True)
    flat_back = returned.reshape(expert_count * slot_count, model_width)
    picked = flat_back[jnp.minimum(buffer_index, expert_count * slot_count - 1)]
    weights = jnp.where(usable, gate_probs.reshape(-1), 0.0)
    mixed = picked.astype(jnp.float32) * weights[:, None]
    return mixed.reshape(tok_rows, top_count, model_width).sum(axis=1).astype(jnp.bfloat16)


def solution(mesh):
    split = Mesh(
        mesh.devices.reshape(mesh.shape["attn"], 4, 4, 2),
        ("attn", "expert_0", "expert_1", "expert_2"),
    )
    return jax.shard_map(
        on_device,
        mesh=split,
        in_specs=(
            P(ATTN_EXPERT, None),
            P(ATTN_EXPERT, None),
            P(ATTN_EXPERT, None),
            P(),
            P(),
            P(EXPERT, None, "attn"),
            P(EXPERT, None, "attn"),
            P(EXPERT, "attn", None),
        ),
        out_specs=P(ATTN_EXPERT, None),
        check_vma=False,
    )
```

profile of v0, /device:TPU:0, one launch (start us, length us, event | category | flops | bytes accessed | tf_op | source)
XLA Modules:
  0.0 470.4 jit_solution(2602426872722942839)
XLA Ops:
  6.5 0.8 copy.21
  7.7 1.2 dynamic-slice
  9.9 1.8 all-reduce
  11.7 1.2 dynamic-slice.1
  13.7 9.2 %all-reduce.1 = s32[128]{0:T(128)S(1)} all-reduce(s32[128]{0:T(128)S(1)} %fusion.33), channel_id=3, replica_groups=mesh['attn'=4,'expert_0'=4,'expert_1'=4,'expert_2'=2] {'expert_1'}, use_global_device_ids=true, to_apply=%add.1 | all-reduce | flops 128 | bytes 1024
  23.0 11.0 %all-gather.2 = s32[4,1,32]{2,1,0:T(1,128)S(1)} all-gather(s32[1,1,32]{2,1,0:T(1,128)S(1)} %fusion.37), channel_id=1, replica_groups=mesh['attn'=4,'expert_0'=4,'expert_1'=4,'expert_2'=2] {'expert_0'}, dimensions={0}, use_global_device_ids=true | all-gather | bytes 640 | tf_op jit(solution)/shard_map/all_gather | solution.py:22
  34.0 9.7 %all-gather.3 = s32[4,1,32]{2,1,0:T(1,128)S(1)} all-gather(s32[1,1,32]{2,1,0:T(1,128)S(1)} %slice_add_fusion.3), channel_id=1, replica_groups=mesh['attn'=4,'expert_0'=4,'expert_1'=4,'expert_2'=2] {'attn'}, dimensions={0}, use_global_device_ids=true | all-gather | bytes 640 | tf_op jit(solution)/shard_map/all_gather | solution.py:22
  43.9 0.8 select_reduce_fusion.5
  44.8 0.9 select_reduce_fusion.1
  46.2 1.0 scatter_custom_fusion
  47.2 0.7 all_to_all.15
  47.9 3.8 all-to-all-start
  51.7 1.1 broadcast_in_dim.80
  53.2 4.6 scatter_custom_fusion.1
  57.7 1.3 all-to-all-done
  59.0 6.2 %all-to-all-start.1 = ((bf16[32,24,2880]{2,1,0:T(8,128)(2,1)}), bf16[32,24,2880]{2,1,0:T(8,128)(2,1)}, u32[]{:S(2)}, u32[]{:S(2)}) async-start(bf16[32,24,2880]{2,1,0:T(8,128)(2,1)} %bitcast.70), calls=%async_computation.1 | async-start | bytes 9043968 | tf_op jit(solution)/shard_map/all_to_all | solution.py:106
  66.0 0.7 broadcast_minimum_fusion
  66.8 56.1 %all-to-all-done.1 = bf16[32,24,2880]{2,1,0:T(8,128)(2,1)} async-done(((bf16[32,24,2880]{2,1,0:T(8,128)(2,1)}), bf16[32,24,2880]{2,1,0:T(8,128)(2,1)}, u32[]{:S(2)}, u32[]{:S(2)}) %all-to-all-start.1) | async-done | bytes 4423712 | tf_op jit(solution)/shard_map/all_to_all | solution.py:106
  122.9 13.9 %scatter_custom_fusion.2 = f32[768,2880]{1,0:T(8,128)} fusion(s32[768]{0:T(1024)S(1)} %fusion.20, bf16[768,2880]{1,0:T(8,128)(2,1)} %bitcast.25, f32[]{:T(128)} %constant.17.clone.1), kind=kCustom, calls=%fused_computation.5 | custom fusion | flops 2211840 | bytes 13271044 | tf_op jit(solution)/shard_map/scatter | solution.py:112
  136.8 6.2 %convert_element_type.37 = bf16[768,2880]{1,0:T(8,128)(2,1)} convert(f32[768,2880]{1,0:T(8,128)} %scatter_custom_fusion.2) | non-fusion elementwise | flops 2211840 | bytes 13271040 | tf_op jit(solution)/shard_map/convert_element_type | solution.py:114
  143.3 92.2 %all-reduce.4.cloned.1.call-done = bf16[768,2880]{1,0:T(8,128)(2,1)} async-done(((bf16[768,2880]{1,0:T(8,128)(2,1)}), bf16[768,2880]{1,0:T(8,128)(2,1)}) %all-reduce.4.cloned.1.call-update) | async-done | bytes 4423696 | tf_op jit(solution)/shard_map/psum | solution.py:114
  235.5 8.6 %fusion.4 = f32[768,720]{0,1:T(8,128)} fusion(bf16[768,2880]{1,0:T(8,128)(2,1)} %all-reduce.4.cloned.1.call-done, bf16[1,2880,720]{1,2,0:T(8,128)(2,1)} %param.14), kind=kOutput, calls=%fused_computation.10 | convolution fusion | flops 3185049600 | bytes 10782720 | tf_op jit(solution)/shard_map/dot_general | solution.py:55
  244.1 15.6 %convolution_convert_fusion = bf16[768,2880]{0,1:T(8,128)(2,1)} fusion(bf16[1,720,2880]{2,1,0:T(8,128)(2,1)} %param.15, f32[768,720]{0,1:T(8,128)} %fusion.4, bf16[768,2880]{1,0:T(8,128)(2,1)} %all-reduce.4.cloned.1.call-done, bf16[1,2880,720]{1,2,0:T(8,128)(2,1)} %param.13), kind=kOutput, calls=%fused_computation.7 | convolution fusion | flops 6376734720 | bytes 19353600 | tf_op jit(solution)/shard_map/dot_general | solution.py:120
  259.7 6.5 %copy.24 = bf16[768,2880]{1,0:T(8,128)(2,1)} copy(bf16[768,2880]{0,1:T(8,128)(2,1)} %convolution_convert_fusion) | data formatting | bytes 8847360 | tf_op jit(solution)/shard_map/convert_element_type | solution.py:120
  266.2 58.4 %all_to_all.24 = bf16[4,192,2880]{2,1,0:T(8,128)(2,1)} all-to-all(bf16[4,192,2880]{2,1,0:T(8,128)(2,1)} %bitcast.71), channel_id=1, replica_groups=mesh['attn'=4,'expert_0'=4,'expert_1'=4,'expert_2'=2] {'attn'}, dimensions={0} | all-to-all | bytes 8847360 | tf_op jit(solution)/shard_map/all_to_all | solution.py:40
  324.6 4.3 reduce_sum.99
  329.0 50.4 %all-gather.6.cloned.1.call-done = bf16[768,2880]{1,0:T(8,128)(2,1)} async-done(((bf16[192,2880]{1,0:T(8,128)(2,1)}), bf16[768,2880]{1,0:T(8,128)(2,1)}) %all-gather.6.cloned.1.call-update) | async-done | bytes 4423696 | tf_op jit(solution)/shard_map/all_gather | solution.py:124
  379.4 12.2 %gather_fusion = bf16[768,2880]{1,0:T(8,128)(2,1)} fusion(bf16[768,2880]{1,0:T(8,128)(2,1)} %all-gather.6.cloned.1.call-done, s32[1024]{0:T(1024)S(1)} %pad_clamp_fusion.1), kind=kCustom, calls=%fused_computation | custom fusion | bytes 8850432 | tf_op jit(solution)/shard_map/gather | solution.py:125
  391.7 7.5 %all-to-all-start.3 = ((bf16[32,24,2880]{2,1,0:T(8,128)(2,1)}), bf16[32,24,2880]{2,1,0:T(8,128)(2,1)}, u32[]{:S(2)}, u32[]{:S(2)}) async-start(bf16[32,24,2880]{2,1,0:T(8,128)(2,1)} %bitcast.69), calls=%async_computation.3 | async-start | bytes 9043968 | tf_op jit(solution)/shard_map/all_to_all | solution.py:126
  399.6 57.2 %all-to-all-done.3 = bf16[32,24,2880]{2,1,0:T(8,128)(2,1)} async-done(((bf16[32,24,2880]{2,1,0:T(8,128)(2,1)}), bf16[32,24,2880]{2,1,0:T(8,128)(2,1)}, u32[]{:S(2)}, u32[]{:S(2)}) %all-to-all-start.3) | async-done | bytes 4423712 | tf_op jit(solution)/shard_map/all_to_all | solution.py:126
  456.8 4.7 gather_fusion.1
  461.9 1.7 multiply_reduce_fusion
  (39 shorter events, 4.0 us)
Async XLA Ops:
  47.9 11.1 %all-to-all-start = ((s32[32,1,24]{2,1,0:T(1,128)}), s32[32,1,24]{2,1,0:T(1,128)S(1)}, u32[]{:S(2)}, u32[]{:S(2)}) async-start(s32[32,1,24]{2,1,0:T(1,128)} %bitcast.14), calls=%async_computation | async-start | bytes 32768 | tf_op jit(solution)/shard_map/all_to_all | solution.py:107
  59.0 63.9 %all-to-all-start.1 = ((bf16[32,24,2880]{2,1,0:T(8,128)(2,1)}), bf16[32,24,2880]{2,1,0:T(8,128)(2,1)}, u32[]{:S(2)}, u32[]{:S(2)}) async-start(bf16[32,24,2880]{2,1,0:T(8,128)(2,1)} %bitcast.70), calls=%async_computation.1 | async-start | bytes 9043968 | tf_op jit(solution)/shard_map/all_to_all | solution.py:106
  65.2 170.3 %all-reduce.4.cloned.1.call-start = ((), (), s32[]{:S(2)}) async-start(), calls=%async_computation.4 | async-start | bytes 9043968 | tf_op jit(solution)/shard_map/psum | solution.py:114
  143.0 236.4 %all-gather.6.cloned.1.call-start = ((), (), s32[]{:S(2)}) async-start(), calls=%async_computation.5 | async-start | bytes 5652480 | tf_op jit(solution)/shard_map/all_gather | solution.py:124
  391.6 7.8 %copy-start = (f32[32,4]{0,1:T(4,128)S(1)}, f32[32,4]{0,1:T(4,128)}, u32[]{:S(2)}) copy-start(f32[32,4]{0,1:T(4,128)} %param.10) | copy-start | bytes 1540
  391.7 65.2 %all-to-all-start.3 = ((bf16[32,24,2880]{2,1,0:T(8,128)(2,1)}), bf16[32,24,2880]{2,1,0:T(8,128)(2,1)}, u32[]{:S(2)}, u32[]{:S(2)}) async-start(bf16[32,24,2880]{2,1,0:T(8,128)(2,1)} %bitcast.69), calls=%async_computation.3 | async-start | bytes 9043968 | tf_op jit(solution)/shard_map/all_to_all | solution.py:126
Sparse Core Ops, SparseCore 0:
  143.2 92.3 all-reduce.3
  329.0 50.3 all-gather.5
where the time goes:
time: 471 us; the launch traced here: 470 us
  waiting for transfers between devices  257 us (55%)
  blocking collectives  90.1 us (19%)
  local copies, waits for them, and re-layouts  36.3 us (8%)
  other arithmetic  29.7 us (6%)
  matrix products  24.2 us (5%)
  starting transfers between devices  18.1 us (4%)
  between operations  14.9 us (3%)
    psum x1, waiting for transfers between devices, on_device(): compact = lax.psum(local_table.astype(jnp.bfloat16), 'attn')  92.2 us
    all_to_all x1, blocking collectives, sum_at_owner(): lax.all_to_all(parts, axis, split_axis=0, concat_axis=0, tiled=True)  58.4 us
    all_to_all x1, waiting for transfers between devices, on_device(): lax.all_to_all(answers, EXPERT, split_axis=0, concat_axis=0, tiled=True)  57.2 us
    all_to_all x1, waiting for transfers between devices, on_device(): lax.all_to_all(send_rows, EXPERT, split_axis=0, concat_axis=0, tiled=True)  56.1 us
    all_gather x1, waiting for transfers between devices, on_device(): lax.all_gather(share.astype(jnp.bfloat16), 'attn', axis=0, tiled=True)  50.4 us
    all_gather x2, blocking collectives, prefix_by_axis(): pieces = lax.all_gather(total, axis)  20.7 us
    dot_general x1, matrix products, on_device(): jnp.dot(hidden_own, down_own, preferred_element_type=jnp.float32)  15.6 us
    scatter x1, other arithmetic, on_device(): local_table = jnp.zeros((table_rows, model_width), jnp.float32).at[got_sl...  13.9 us
  transfers between devices with their start and end apart: 5, of which 5 were waited for; matrix products, arithmetic and copies ran while one was open for 2% of the time, Pallas kernels for 0%

commit v1 on v0

--- a/solution.py
+++ b/solution.py
@@ -8,6 +8,27 @@
 ATTN_EXPERT = ("attn", "expert_0", "expert_1", "expert_2")
 EXPERT = ("expert_0", "expert_1", "expert_2")
 SWISH_SCALE = 1.702
+
+
+def ring_gather(array, axis, dim):
+    count, index, extent = (lax.axis_size(axis), lax.axis_index(axis), array.shape[dim])
+    upward = [(i, (i + 1) % count) for i in range(count)]
+    left = [(i, (i - 1) % count) for i in range(count)]
+    out = jnp.zeros((*array.shape[:dim], count * extent, *array.shape[dim + 1 :]), array.dtype)
+    out = lax.dynamic_update_slice_in_dim(out, array, index * extent, axis=dim)
+    from_left = from_right = array
+    halfway = count // 2
+    for step in range(1, halfway + 1):
+        from_left = lax.ppermute(from_left, axis, upward)
+        out = lax.dynamic_update_slice_in_dim(
+            out, from_left, (index - step) % count * extent, axis=dim
+        )
+        if step < count - halfway:
+            from_right = lax.ppermute(from_right, axis, left)
+            out = lax.dynamic_update_slice_in_dim(
+                out, from_right, (index + step) % count * extent, axis=dim
+            )
+    return out
 
 
 def nothing_yet(array, identity):
@@ -121,7 +142,7 @@
         "attn",
         0,
     )
-    results = lax.all_gather(share.astype(jnp.bfloat16), "attn", axis=0, tiled=True)
+    results = ring_gather(share.astype(jnp.bfloat16), "attn", 0)
     answers = results[jnp.minimum(got_slots, table_rows - 1)]
     returned = lax.all_to_all(answers, EXPERT, split_axis=0, concat_axis=0, tiled=True)
     flat_back = returned.reshape(expert_count * slot_count, model_width)

time: 471 us -> 471 us (level)
  local copies, waits for them, and re-layouts: 36.3 us -> 43.1 us
  waiting for transfers between devices: 257 us -> 251 us
    all_gather x1 -> x0, waiting for transfers between devices: 50.4 us -> none  [on_device(): lax.all_gather(share.astype(jnp.bfloat16), 'attn', axis=0, tiled=True)]
    ppermute x0 -> x3, waiting for transfers between devices: none -> 43.6 us  [the longest x2 43.6 us: ring_gather(): from_left = lax.ppermute(from_left, axis, upward)]
  transfers between devices with their start and end apart: 5 -> 7, of which waited for: 5 -> 6; matrix products, arithmetic and copies ran while one was open for 2% -> 3% of each run, Pallas kernels for 0% -> 0%
where the time goes in v1:
time: 471 us
  waiting for transfers between devices  251 us (53%)
  blocking collectives  90.1 us (19%)
  local copies, waits for them, and re-layouts  43.1 us (9%)
  other arithmetic  28.9 us (6%)
  matrix products  21.7 us (5%)
  starting transfers between devices  21.1 us (4%)
  between operations  14.9 us (3%)
    psum x1, waiting for transfers between devices, on_device(): compact = lax.psum(local_table.astype(jnp.bfloat16), 'attn')  92.5 us
    all_to_all x1, blocking collectives, sum_at_owner(): lax.all_to_all(parts, axis, split_axis=0, concat_axis=0, tiled=True)  58.4 us
    all_to_all x1, waiting for transfers between devices, on_device(): lax.all_to_all(answers, EXPERT, split_axis=0, concat_axis=0, tiled=True)  57.2 us
    all_to_all x1, waiting for transfers between devices, on_device(): lax.all_to_all(send_rows, EXPERT, split_axis=0, concat_axis=0, tiled=True)  56.1 us
    ppermute x2, waiting for transfers between devices, ring_gather(): from_left = lax.ppermute(from_left, axis, upward)  43.6 us
    all_gather x2, blocking collectives, prefix_by_axis(): pieces = lax.all_gather(total, axis)  20.7 us
    dot_general x1, matrix products, on_device(): jnp.dot(hidden_own, down_own, preferred_element_type=jnp.float32)  14.9 us
    scatter x1, other arithmetic, on_device(): local_table = jnp.zeros((table_rows, model_width), jnp.float32).at[got_sl...  13.9 us
  transfers between devices with their start and end apart: 7, of which 6 were waited for; matrix products, arithmetic and copies ran while one was open for 3% of the time, Pallas kernels for 0%

profile of v1, /device:TPU:0, one launch (start us, length us, event | category | flops | bytes accessed | tf_op | source)
XLA Modules:
  0.0 470.5 jit_solution(16814677028537731703)
XLA Ops:
  7.7 1.2 dynamic-slice
  9.9 1.8 all-reduce
  11.7 1.2 dynamic-slice.1
  13.7 9.2 %all-reduce.1 = s32[128]{0:T(128)S(1)} all-reduce(s32[128]{0:T(128)S(1)} %fusion.33), channel_id=3, replica_groups=mesh['attn'=4,'expert_0'=4,'expert_1'=4,'expert_2'=2] {'expert_1'}, use_global_device_ids=true, to_apply=%add.1 | all-reduce | flops 128 | bytes 1024
  23.0 11.0 %all-gather.2 = s32[4,1,32]{2,1,0:T(1,128)S(1)} all-gather(s32[1,1,32]{2,1,0:T(1,128)S(1)} %fusion.37), channel_id=1, replica_groups=mesh['attn'=4,'expert_0'=4,'expert_1'=4,'expert_2'=2] {'expert_0'}, dimensions={0}, use_global_device_ids=true | all-gather | bytes 640 | tf_op jit(solution)/shard_map/all_gather | solution.py:43
  34.0 9.7 %all-gather.3 = s32[4,1,32]{2,1,0:T(1,128)S(1)} all-gather(s32[1,1,32]{2,1,0:T(1,128)S(1)} %slice_add_fusion.3), channel_id=1, replica_groups=mesh['attn'=4,'expert_0'=4,'expert_1'=4,'expert_2'=2] {'attn'}, dimensions={0}, use_global_device_ids=true | all-gather | bytes 640 | tf_op jit(solution)/shard_map/all_gather | solution.py:43
  47.9 3.8 all-to-all-start
  51.7 1.1 broadcast_in_dim.76
  53.2 4.6 scatter_custom_fusion.1
  57.7 1.3 all-to-all-done
  59.0 6.2 %all-to-all-start.1 = ((bf16[32,24,2880]{2,1,0:T(8,128)(2,1)}), bf16[32,24,2880]{2,1,0:T(8,128)(2,1)}, u32[]{:S(2)}, u32[]{:S(2)}) async-start(bf16[32,24,2880]{2,1,0:T(8,128)(2,1)} %bitcast.70), calls=%async_computation.1 | async-start | bytes 9043968 | tf_op jit(solution)/shard_map/all_to_all | solution.py:127
  66.8 56.1 %all-to-all-done.1 = bf16[32,24,2880]{2,1,0:T(8,128)(2,1)} async-done(((bf16[32,24,2880]{2,1,0:T(8,128)(2,1)}), bf16[32,24,2880]{2,1,0:T(8,128)(2,1)}, u32[]{:S(2)}, u32[]{:S(2)}) %all-to-all-start.1) | async-done | bytes 4423712 | tf_op jit(solution)/shard_map/all_to_all | solution.py:127
  122.9 13.9 %scatter_custom_fusion.2 = f32[768,2880]{1,0:T(8,128)} fusion(s32[768]{0:T(1024)S(1)} %fusion.20, bf16[768,2880]{1,0:T(8,128)(2,1)} %bitcast.25, f32[]{:T(128)} %constant.33.clone.1), kind=kCustom, calls=%fused_computation.5 | custom fusion | flops 2211840 | bytes 13271044 | tf_op jit(solution)/shard_map/scatter | solution.py:133
  136.8 6.2 %convert_element_type.37 = bf16[768,2880]{1,0:T(8,128)(2,1)} convert(f32[768,2880]{1,0:T(8,128)} %scatter_custom_fusion.2) | non-fusion elementwise | flops 2211840 | bytes 13271040 | tf_op jit(solution)/shard_map/convert_element_type | solution.py:135
  143.0 92.5 %all-reduce.4.cloned.1.call-done = bf16[768,2880]{1,0:T(8,128)(2,1)} async-done(((bf16[768,2880]{1,0:T(8,128)(2,1)}), bf16[768,2880]{1,0:T(8,128)(2,1)}) %all-reduce.4.cloned.1.call-update) | async-done | bytes 4423696 | tf_op jit(solution)/shard_map/psum | solution.py:135
  235.5 6.8 %fusion.4 = f32[768,720]{0,1:T(8,128)S(1)} fusion(bf16[768,2880]{1,0:T(8,128)(2,1)} %all-reduce.4.cloned.1.call-done, bf16[1,2880,720]{1,2,0:T(8,128)(2,1)} %param.14), kind=kOutput, calls=%fused_computation.10 | convolution fusion | flops 3185049600 | bytes 10782720 | tf_op jit(solution)/shard_map/dot_general | solution.py:76
  242.3 14.9 %convolution_convert_fusion = bf16[768,2880]{0,1:T(8,128)(2,1)} fusion(bf16[1,720,2880]{2,1,0:T(8,128)(2,1)} %param.15, f32[768,720]{0,1:T(8,128)S(1)} %fusion.4, bf16[768,2880]{1,0:T(8,128)(2,1)} %all-reduce.4.cloned.1.call-done, bf16[1,2880,720]{1,2,0:T(8,128)(2,1)} %param.13), kind=kOutput, calls=%fused_computation.7 | convolution fusion | flops 6376734720 | bytes 19353600 | tf_op jit(solution)/shard_map/dot_general | solution.py:141
  257.2 6.5 %copy.24 = bf16[768,2880]{1,0:T(8,128)(2,1)} copy(bf16[768,2880]{0,1:T(8,128)(2,1)} %convolution_convert_fusion) | data formatting | bytes 8847360 | tf_op jit(solution)/shard_map/convert_element_type | solution.py:141
  263.7 58.4 %all_to_all.24 = bf16[4,192,2880]{2,1,0:T(8,128)(2,1)} all-to-all(bf16[4,192,2880]{2,1,0:T(8,128)(2,1)} %bitcast.71), channel_id=1, replica_groups=mesh['attn'=4,'expert_0'=4,'expert_1'=4,'expert_2'=2] {'attn'}, dimensions={0} | all-to-all | bytes 8847360 | tf_op jit(solution)/shard_map/all_to_all | solution.py:61
  322.1 3.5 reduce_sum.99
  326.3 2.7 collective-permute-start.1
  329.0 23.5 %collective-permute-done = bf16[192,2880]{1,0:T(8,128)(2,1)S(1)} collective-permute-done((bf16[192,2880]{1,0:T(8,128)(2,1)S(1)}, bf16[192,2880]{1,0:T(8,128)(2,1)S(1)}, u32[]{:S(2)}, u32[]{:S(2)}) %collective-permute-start) | collective-permute-done | bytes 1105952 | tf_op jit(solution)/shard_map/ppermute | solution.py:22
  352.6 2.4 broadcast.186
  355.0 1.1 constant_dynamic-update-slice_fusion.3
  356.1 1.2 constant_dynamic-update-slice_fusion.2
  357.3 1.1 constant_dynamic-update-slice_fusion.1
  358.4 20.1 %collective-permute-done.2 = bf16[192,2880]{1,0:T(8,128)(2,1)S(1)} collective-permute-done((bf16[192,2880]{1,0:T(8,128)(2,1)S(1)}, bf16[192,2880]{1,0:T(8,128)(2,1)S(1)}, u32[]{:S(2)}, u32[]{:S(2)}) %collective-permute-start.2) | collective-permute-done | bytes 1105952 | tf_op jit(solution)/shard_map/ppermute | solution.py:22
  379.6 12.2 %gather_fusion = bf16[768,2880]{1,0:T(8,128)(2,1)} fusion(bf16[768,2880]{1,0:T(8,128)(2,1)} %constant_dynamic-update-slice_fusion, s32[1024]{0:T(1024)S(1)} %pad_clamp_fusion.1), kind=kCustom, calls=%fused_computation | custom fusion | bytes 8850432 | tf_op jit(solution)/shard_map/gather | solution.py:146
  391.7 7.5 %all-to-all-start.3 = ((bf16[32,24,2880]{2,1,0:T(8,128)(2,1)}), bf16[32,24,2880]{2,1,0:T(8,128)(2,1)}, u32[]{:S(2)}, u32[]{:S(2)}) async-start(bf16[32,24,2880]{2,1,0:T(8,128)(2,1)} %bitcast.69), calls=%async_computation.3 | async-start | bytes 9043968 | tf_op jit(solution)/shard_map/all_to_all | solution.py:147
  399.7 57.2 %all-to-all-done.3 = bf16[32,24,2880]{2,1,0:T(8,128)(2,1)} async-done(((bf16[32,24,2880]{2,1,0:T(8,128)(2,1)}), bf16[32,24,2880]{2,1,0:T(8,128)(2,1)}, u32[]{:S(2)}, u32[]{:S(2)}) %all-to-all-start.3) | async-done | bytes 4423712 | tf_op jit(solution)/shard_map/all_to_all | solution.py:147
  456.9 4.7 gather_fusion.1
  462.0 1.7 multiply_reduce_fusion
  (47 shorter events, 10.2 us)
Async XLA Ops:
  47.9 11.1 %all-to-all-start = ((s32[32,1,24]{2,1,0:T(1,128)}), s32[32,1,24]{2,1,0:T(1,128)S(1)}, u32[]{:S(2)}, u32[]{:S(2)}) async-start(s32[32,1,24]{2,1,0:T(1,128)} %bitcast.14), calls=%async_computation | async-start | bytes 32768 | tf_op jit(solution)/shard_map/all_to_all | solution.py:128
  59.0 63.9 %all-to-all-start.1 = ((bf16[32,24,2880]{2,1,0:T(8,128)(2,1)}), bf16[32,24,2880]{2,1,0:T(8,128)(2,1)}, u32[]{:S(2)}, u32[]{:S(2)}) async-start(bf16[32,24,2880]{2,1,0:T(8,128)(2,1)} %bitcast.70), calls=%async_computation.1 | async-start | bytes 9043968 | tf_op jit(solution)/shard_map/all_to_all | solution.py:127
  65.2 170.3 %all-reduce.4.cloned.1.call-start = ((), (), s32[]{:S(2)}) async-start(), calls=%async_computation.4 | async-start | bytes 9043968 | tf_op jit(solution)/shard_map/psum | solution.py:135
  325.6 26.9 %collective-permute-start = (bf16[192,2880]{1,0:T(8,128)(2,1)S(1)}, bf16[192,2880]{1,0:T(8,128)(2,1)S(1)}, u32[]{:S(2)}, u32[]{:S(2)}) collective-permute-start(bf16[192,2880]{1,0:T(8,128)(2,1)S(1)} %reduce_sum.99), channel_id=1, source_target_pairs={{0,32},{32,64},{64,96},{96,0},{1,33},{33,65},{65,97},{97,1},{2,34}... | collective-permute-start | bytes 3317768 | tf_op jit(solution)/shard_map/ppermute | solution.py:22
  326.3 31.0 %collective-permute-start.1 = (bf16[192,2880]{1,0:T(8,128)(2,1)S(1)}, bf16[192,2880]{1,0:T(8,128)(2,1)S(1)}, u32[]{:S(2)}, u32[]{:S(2)}) collective-permute-start(bf16[192,2880]{1,0:T(8,128)(2,1)S(1)} %reduce_sum.99), channel_id=1, source_target_pairs={{0,96},{32,0},{64,32},{96,64},{1,97},{33,1},{65,33},{97,65},{2,98}... | collective-permute-start | bytes 3317768 | tf_op jit(solution)/shard_map/ppermute | solution.py:27
  352.5 26.0 %collective-permute-start.2 = (bf16[192,2880]{1,0:T(8,128)(2,1)S(1)}, bf16[192,2880]{1,0:T(8,128)(2,1)S(1)}, u32[]{:S(2)}, u32[]{:S(2)}) collective-permute-start(bf16[192,2880]{1,0:T(8,128)(2,1)S(1)} %collective-permute-done), channel_id=1, source_target_pairs={{0,32},{32,64},{64,96},{96,0},{1,33},{33,65},{65,97},{97,1},{2,34}... | collective-permute-start | bytes 3317768 | tf_op jit(solution)/shard_map/ppermute | solution.py:22
  391.7 7.9 %copy-start = (f32[32,4]{0,1:T(4,128)S(1)}, f32[32,4]{0,1:T(4,128)}, u32[]{:S(2)}) copy-start(f32[32,4]{0,1:T(4,128)} %param.10) | copy-start | bytes 1540
  391.7 65.2 %all-to-all-start.3 = ((bf16[32,24,2880]{2,1,0:T(8,128)(2,1)}), bf16[32,24,2880]{2,1,0:T(8,128)(2,1)}, u32[]{:S(2)}, u32[]{:S(2)}) async-start(bf16[32,24,2880]{2,1,0:T(8,128)(2,1)} %bitcast.69), calls=%async_computation.3 | async-start | bytes 9043968 | tf_op jit(solution)/shard_map/all_to_all | solution.py:147
Sparse Core Ops, SparseCore 0:
  143.2 92.3 all-reduce.3
